TPU v7x, 32 devices: a whole 2x2x4 slice. The times are simulated.
32 devices in a mesh: px: 4 (over z), py: 4 (over y, x), pz: 2 (over core).
Axes of the slice: x: 2, y: 2, z: 4, core: 2. Of those that a mesh axis runs over, the one named last changes fastest.
Arguments:
- right_side: float32 [16, 64, 256], P('px', 'py', 'pz'), may hold values from -160 to 160
- start_guess: float32 [16, 64, 256], P('px', 'py', 'pz'), may hold values from -4 to 4
- conductivity: float32 [16, 64, 256], P('px', 'py', 'pz'), may hold values from 0.05 to 0.4
- recycled: float32 [16, 16, 64, 256], P(None, 'px', 'py', 'pz'), may hold values from -6 to 6
Outputs:
- solution: float32 [16, 64, 256], P('px', 'py', 'pz')
- residual: float32 [16, 64, 256], P('px', 'py', 'pz')
- hessenberg: float32 [9, 8], replicated
All inputs are finite; a program needn't handle non-finite values.
Results may differ from a plain program's by a relative error of at most 0.03.
Values sent between devices are 32-bit elements; how exact they have to be, the bound alone decides.
A program may use at most 128 MiB of HBM per device.

v0:
```python
import jax
import jax.numpy as jnp
from jax import lax
from jax.sharding import PartitionSpec as P

STEPS = 8


highest = lax.Precision.HIGHEST
edge_weight = 0.25 ** (1.0 / 3.0)
middle_weight = 2.0 * edge_weight
shift_value = 0.4


def padded_2(array, sides, width):
    for axis, dim in sides:
        peers, length = (lax.axis_size(axis), array.shape[dim])
        up = [(i, (i + 1) % peers) for i in range(peers - 1)]
        down = [(j, i) for i, j in up]
        last = lax.slice_in_dim(array, length - width, length, axis=dim)
        leading = lax.slice_in_dim(array, 0, width, axis=dim)
        before = lax.ppermute(last, axis, up)
        after = lax.ppermute(leading, axis, down)
        array = jnp.concatenate([before, array, after], axis=dim)
    return array


def stencil_sum(padded):
    along_z = edge_weight * (padded[..., :-2] + padded[..., 2:]) + middle_weight * padded[..., 1:-1]
    along_y = (
        edge_weight * (along_z[..., :-2, :] + along_z[..., 2:, :])
        + middle_weight * along_z[..., 1:-1, :]
    )
    along_x = (
        edge_weight * (along_y[..., :-2, :, :] + along_y[..., 2:, :, :])
        + middle_weight * along_y[..., 1:-1, :, :]
    )
    return along_x - 2.0 * padded[..., 1:-1, 1:-1, 1:-1]


def apply_batch(fields, conductivity, diagonal):
    stacked = jnp.concatenate((fields, conductivity[None] * fields), axis=0)
    padded = padded_2(stacked, (("px", 1), ("py", 2), ("pz", 3)), 1)
    half_count = fields.shape[0]
    near_sum = stencil_sum(padded[:half_count])
    far_sum = stencil_sum(padded[half_count:])
    return diagonal * fields - 0.5 * conductivity * near_sum - 0.5 * far_sum


def apply_vector(fields, conductivity, diagonal):
    stacked = jnp.concatenate((fields, conductivity[None] * fields), axis=0)
    padded = padded_2(stacked, (("px", 1), ("py", 2), ("pz", 3)), 1)
    near_sum = stencil_sum(padded[:1])
    far_sum = stencil_sum(padded[1:])
    return diagonal * fields - 0.5 * conductivity * near_sum - 0.5 * far_sum


def cholesky_low(gram):
    order = gram.shape[0]
    rows_idx = jnp.arange(order)
    factor = jnp.zeros((order, order), jnp.float32)
    for column in range(order):
        known = factor[:, :column]
        partial_sum = jnp.sum(known * known[column][None, :], axis=1)
        pivot = jnp.sqrt(gram[column, column] - partial_sum[column])
        values = (gram[:, column] - partial_sum) / pivot
        values = jnp.where(rows_idx > column, values, 0.0)
        factor = factor.at[:, column].set(values).at[column, column].set(pivot)
    return factor


def lower_inverse(factor):
    order = factor.shape[0]
    inverse = jnp.zeros((order, order), jnp.float32)
    for row in range(order):
        unit_row = jnp.zeros((order,), jnp.float32).at[row].set(1.0)
        partial_value = jnp.sum(factor[row, :row][:, None] * inverse[:row], axis=0)
        inverse = inverse.at[row].set((unit_row - partial_value) / factor[row, row])
    return inverse


def back_solve(upper_tri, target):
    order = upper_tri.shape[0]
    result = jnp.zeros((order,), jnp.float32)
    for row in range(order - 1, -1, -1):
        partial_value = jnp.sum(upper_tri[row, row + 1 :] * result[row + 1 :])
        result = result.at[row].set((target[row] - partial_value) / upper_tri[row, row])
    return result


def least_squares(hessenberg, beta_norm):
    upper_tri = hessenberg
    target = jnp.zeros((STEPS + 1,), jnp.float32).at[0].set(beta_norm)
    for column in range(STEPS):
        top_entry = upper_tri[column, column]
        low_entry = upper_tri[column + 1, column]
        radius = jnp.sqrt(top_entry * top_entry + low_entry * low_entry)
        cosine = top_entry / radius
        sine_val = low_entry / radius
        row_top = cosine * upper_tri[column] + sine_val * upper_tri[column + 1]
        row_low = cosine * upper_tri[column + 1] - sine_val * upper_tri[column]
        upper_tri = upper_tri.at[column].set(row_top).at[column + 1].set(row_low)
        goal_top = cosine * target[column] + sine_val * target[column + 1]
        goal_low = cosine * target[column + 1] - sine_val * target[column]
        target = target.at[column].set(goal_top).at[column + 1].set(goal_low)
    return back_solve(upper_tri[:STEPS], target[:STEPS])


def body(right_side, start_guess, conductivity, recycled):
    count_k = recycled.shape[0]
    block_shape = right_side.shape
    cell_count = right_side.size
    padded_cond = padded_2(conductivity, (("px", 0), ("py", 1), ("pz", 2)), 1)
    diagonal = shift_value + 7.0 * conductivity + 0.5 * stencil_sum(padded_cond)
    batch_in = jnp.concatenate((recycled, start_guess[None]), axis=0)
    images_all = apply_batch(batch_in, conductivity, diagonal)
    flat_images = images_all[:count_k].reshape(count_k, cell_count)
    first_residual = right_side.reshape(cell_count) - images_all[count_k].reshape(cell_count)
    gram = lax.psum(jnp.dot(flat_images, flat_images.T, precision=highest), ("px", "py", "pz"))
    factor_low = cholesky_low(gram)
    inverse = lower_inverse(factor_low)
    basis_c = jnp.dot(inverse, flat_images, precision=highest)
    projected = lax.psum(jnp.dot(basis_c, first_residual, precision=highest), ("px", "py", "pz"))
    recycle_flat = recycled.reshape(count_k, cell_count)
    solution = start_guess.reshape(cell_count) + jnp.dot(
        jnp.dot(inverse.T, projected, precision=highest), recycle_flat, precision=highest
    )
    residual = first_residual - jnp.dot(projected, basis_c, precision=highest)
    beta_norm = jnp.sqrt(
        lax.psum(jnp.dot(residual, residual, precision=highest), ("px", "py", "pz"))
    )
    basis_all = jnp.zeros((STEPS + 1, cell_count), jnp.float32).at[0].set(residual / beta_norm)
    coupling = jnp.zeros((count_k, STEPS), jnp.float32)
    hessenberg = jnp.zeros((STEPS + 1, STEPS), jnp.float32)
    for column in range(STEPS):
        current = basis_all[column].reshape((1,) + block_shape)
        vector_new = apply_vector(current, conductivity, diagonal).reshape(cell_count)
        known_basis = basis_all[: column + 1]
        coeff_c, coeff_v, whole_sq = lax.psum(
            (
                jnp.dot(basis_c, vector_new, precision=highest),
                jnp.dot(known_basis, vector_new, precision=highest),
                jnp.dot(vector_new, vector_new, precision=highest),
            ),
            ("px", "py", "pz"),
        )
        vector_new = (
            vector_new
            - jnp.dot(coeff_c, basis_c, precision=highest)
            - jnp.dot(coeff_v, known_basis, precision=highest)
        )
        norm_sq = (
            whole_sq
            - jnp.dot(coeff_c, coeff_c, precision=highest)
            - jnp.dot(coeff_v, coeff_v, precision=highest)
        )
        norm_new = jnp.sqrt(norm_sq)
        coupling = coupling.at[:, column].set(coeff_c)
        hessenberg = hessenberg.at[: column + 1, column].set(coeff_v)
        hessenberg = hessenberg.at[column + 1, column].set(norm_new)
        basis_all = basis_all.at[column + 1].set(vector_new / norm_new)
    coeffs = least_squares(hessenberg, beta_norm)
    recycle_coeffs = jnp.dot(
        inverse.T, jnp.dot(coupling, coeffs, precision=highest), precision=highest
    )
    solution = (
        solution
        + jnp.dot(coeffs, basis_all[:STEPS], precision=highest)
        - jnp.dot(recycle_coeffs, recycle_flat, precision=highest)
    )
    residual = residual - jnp.dot(
        jnp.dot(hessenberg, coeffs, precision=highest), basis_all, precision=highest
    )
    return (solution.reshape(block_shape), residual.reshape(block_shape), hessenberg)


def solution(mesh):
    return jax.shard_map(
        body,
        mesh=mesh,
        in_specs=(
            P("px", "py", "pz"),
            P("px", "py", "pz"),
            P("px", "py", "pz"),
            P(None, "px", "py", "pz"),
        ),
        out_specs=(P("px", "py", "pz"), P("px", "py", "pz"), P()),
        check_vma=False,
    )
```

profile of v0, /device:TPU:0, one launch (start us, length us, event | category | flops | bytes accessed | tf_op | source)
XLA Modules:
  0.0 911.9 jit_solution(14122070898462380592)
XLA Ops:
  3.0 5.0 collective-permute-start.6
  9.3 4.5 collective-permute-start
  19.5 3.4 collective-permute-start.2
  37.9 4.6 collective-permute-start.8
  46.0 5.5 collective-permute-done.9
  52.4 2.7 fusion.321
  55.1 3.1 copy.40
  58.2 2.6 collective-permute-start.10
  60.8 3.1 copy.42
  66.7 3.1 copy.41
  69.8 3.0 copy.43
  72.8 6.4 maximum_maximum_fusion
  82.7 42.2 %psum.189 = f32[16,16]{1,0:T(8,128)S(1)} all-reduce(f32[16,16]{1,0:T(8,128)S(1)} %convolution_bitcast_fusion), channel_id=1, replica_groups=mesh['px'=4,'py'=4,'pz'=2] {'px','py','pz'}, use_global_device_ids=true, to_apply=%region_1.2 | all-reduce | flops 256 | bytes 2048 | tf_op jit(solution)/shard_map/psum | solution.py:119
  187.8 39.8 %psum.190 = f32[16]{0:T(128)S(1)} all-reduce(f32[16]{0:T(128)S(1)} %convolution_bitcast_fusion.20), channel_id=1, replica_groups=mesh['px'=4,'py'=4,'pz'=2] {'px','py','pz'}, use_global_device_ids=true, to_apply=%region_44.45 | all-reduce | flops 16 | bytes 128 | tf_op jit(solution)/shard_map/psum | solution.py:123
  228.6 40.2 %psum.191 = f32[]{:T(128)} all-reduce(f32[]{:T(128)} %get-tuple-element.1699), channel_id=1, replica_groups=mesh['px'=4,'py'=4,'pz'=2] {'px','py','pz'}, use_global_device_ids=true, to_apply=%region_45.46 | all-reduce | flops 1 | bytes 8 | tf_op jit(solution)/shard_map/psum | solution.py:130
  269.5 3.6 collective-permute-start.12
  275.0 3.7 collective-permute-done.13
  278.7 4.2 collective-permute-start.14
  284.3 4.2 collective-permute-done.15
  295.5 40.4 %all-reduce.14 = (f32[16]{0:T(128)S(1)}, f32[]{:T(128)}, f32[1]{0:T(128)}) all-reduce(f32[16]{0:T(128)S(1)} %convolution_bitcast_fusion.19, f32[]{:T(128)} %get-tuple-element.1697, f32[1]{0:T(128)} %bitcast.135), channel_id=1, replica_groups=mesh['px'=4,'py'=4,'pz'=2] {'px','py','pz'}, use_global_device_ids=true, to_apply=%region_48.49 | all-reduce | flops 18 | bytes 144 | tf_op jit(solution)/shard_map/psum | solution.py:139
  344.7 4.2 collective-permute-done.19
  348.9 4.2 collective-permute-start.20
  355.1 3.6 collective-permute-done.21
  365.8 39.3 %all-reduce.13 = (f32[16]{0:T(128)S(1)}, f32[2]{0:T(128)S(1)}, f32[]{:T(128)}) all-reduce(f32[16]{0:T(128)S(1)} %convolution_bitcast_fusion.17, f32[2]{0:T(128)S(1)} %convolution_bitcast_fusion.18, f32[]{:T(128)} %get-tuple-element.1695), channel_id=1, replica_groups=mesh['px'=4,'py'=4,'pz'=2] {'px','py','pz'}, use_global_device_ids=true, to_apply=%region_52.53 | all-reduce | flops 19 | bytes 152 | tf_op jit(solution)/shard_map/psum | solution.py:139
  409.6 3.2 collective-permute-start.24
  414.8 3.7 collective-permute-done.25
  418.5 4.2 collective-permute-start.26
  424.0 4.2 collective-permute-done.27
  435.4 39.3 %all-reduce.12 = (f32[16]{0:T(128)S(1)}, f32[3]{0:T(128)S(1)}, f32[]{:T(128)}) all-reduce(f32[16]{0:T(128)S(1)} %convolution_bitcast_fusion.15, f32[3]{0:T(128)S(1)} %convolution_bitcast_fusion.16, f32[]{:T(128)} %get-tuple-element.1693), channel_id=1, replica_groups=mesh['px'=4,'py'=4,'pz'=2] {'px','py','pz'}, use_global_device_ids=true, to_apply=%region_56.57 | all-reduce | flops 20 | bytes 160 | tf_op jit(solution)/shard_map/psum | solution.py:139
  478.7 3.2 collective-permute-start.30
  483.3 4.2 collective-permute-done.31
  487.5 4.2 collective-permute-start.32
  504.5 41.2 %all-reduce.11 = (f32[16]{0:T(128)S(1)}, f32[4]{0:T(128)S(1)}, f32[]{:T(128)}) all-reduce(f32[16]{0:T(128)S(1)} %convolution_bitcast_fusion.13, f32[4]{0:T(128)S(1)} %convolution_bitcast_fusion.14, f32[]{:T(128)} %get-tuple-element.1691), channel_id=1, replica_groups=mesh['px'=4,'py'=4,'pz'=2] {'px','py','pz'}, use_global_device_ids=true, to_apply=%region_60.61 | all-reduce | flops 21 | bytes 168 | tf_op jit(solution)/shard_map/psum | solution.py:139
  549.6 3.2 collective-permute-start.36
  555.7 2.8 collective-permute-done.37
  558.5 4.2 collective-permute-start.38
  575.3 39.9 %all-reduce.10 = (f32[16]{0:T(128)S(1)}, f32[5]{0:T(128)S(1)}, f32[]{:T(128)}) all-reduce(f32[16]{0:T(128)S(1)} %convolution_bitcast_fusion.11, f32[5]{0:T(128)S(1)} %convolution_bitcast_fusion.12, f32[]{:T(128)} %get-tuple-element.1689), channel_id=1, replica_groups=mesh['px'=4,'py'=4,'pz'=2] {'px','py','pz'}, use_global_device_ids=true, to_apply=%region_64.65 | all-reduce | flops 22 | bytes 176 | tf_op jit(solution)/shard_map/psum | solution.py:139
  619.1 3.2 collective-permute-start.42
  628.0 4.2 collective-permute-start.44
  634.1 3.6 collective-permute-done.45
  646.6 41.4 %all-reduce.9 = (f32[16]{0:T(128)S(1)}, f32[6]{0:T(128)S(1)}, f32[]{:T(128)}) all-reduce(f32[16]{0:T(128)S(1)} %convolution_bitcast_fusion.9, f32[6]{0:T(128)S(1)} %convolution_bitcast_fusion.10, f32[]{:T(128)} %get-tuple-element.1687), channel_id=1, replica_groups=mesh['px'=4,'py'=4,'pz'=2] {'px','py','pz'}, use_global_device_ids=true, to_apply=%region_68.69 | all-reduce | flops 23 | bytes 184 | tf_op jit(solution)/shard_map/psum | solution.py:139
  691.9 2.7 collective-permute-start.48
  696.5 3.7 collective-permute-done.49
  700.2 4.2 collective-permute-start.50
  717.0 40.6 %all-reduce.8 = (f32[16]{0:T(128)S(1)}, f32[7]{0:T(128)S(1)}, f32[]{:T(128)}) all-reduce(f32[16]{0:T(128)S(1)} %convolution_bitcast_fusion.7, f32[7]{0:T(128)S(1)} %convolution_bitcast_fusion.8, f32[]{:T(128)} %get-tuple-element.1685), channel_id=1, replica_groups=mesh['px'=4,'py'=4,'pz'=2] {'px','py','pz'}, use_global_device_ids=true, to_apply=%region_72.73 | all-reduce | flops 24 | bytes 192 | tf_op jit(solution)/shard_map/psum | solution.py:139
  769.8 4.2 collective-permute-start.56
  775.9 3.6 collective-permute-done.57
  788.6 41.4 %all-reduce.7 = (f32[16]{0:T(128)S(1)}, f32[8]{0:T(128)S(1)}, f32[]{:T(128)}) all-reduce(f32[16]{0:T(128)S(1)} %convolution_bitcast_fusion.5, f32[8]{0:T(128)S(1)} %convolution_bitcast_fusion.6, f32[]{:T(128)} %get-tuple-element.1683), channel_id=1, replica_groups=mesh['px'=4,'py'=4,'pz'=2] {'px','py','pz'}, use_global_device_ids=true, to_apply=%region_76.77 | all-reduce | flops 25 | bytes 200 | tf_op jit(solution)/shard_map/psum | solution.py:139
  (649 shorter events, 233.8 us)
Async XLA Ops:
  3.0 34.8 %collective-permute-start.6 = (f32[34,1,16,128]{3,0,2,1:T(8,128)S(1)}, f32[34,1,16,128]{3,0,2,1:T(8,128)S(1)}, u32[]{:S(2)}, u32[]{:S(2)}) collective-permute-start(f32[34,1,16,128]{3,0,2,1:T(8,128)S(1)} %get-tuple-element.1711), channel_id=1, source_target_pairs={{0,8},{8,16},{16,24},{1,9},{9,17},{17,25},{2,10},{10,18},{18,26},{... | collective-permute-start | bytes 835592 | tf_op jit(solution)/shard_map/ppermute | solution.py:22
  8.0 29.9 %collective-permute-start.7 = (f32[34,1,16,128]{3,0,2,1:T(8,128)S(1)}, f32[34,1,16,128]{3,0,2,1:T(8,128)S(1)}, u32[]{:S(2)}, u32[]{:S(2)}) collective-permute-start(f32[34,1,16,128]{3,0,2,1:T(8,128)S(1)} %get-tuple-element.1712), channel_id=1, source_target_pairs={{8,0},{16,8},{24,16},{9,1},{17,9},{25,17},{10,2},{18,10},{26,18},{... | collective-permute-start | bytes 835592 | tf_op jit(solution)/shard_map/ppermute | solution.py:23
  9.3 10.0 %collective-permute-start = (f32[1,16,128]{2,1,0:T(8,128)S(1)}, f32[1,16,128]{2,1,0:T(8,128)S(1)}, u32[]{:S(2)}, u32[]{:S(2)}) collective-permute-start(f32[1,16,128]{2,1,0:T(8,128)S(1)} %get-tuple-element.1768), channel_id=1, source_target_pairs={{0,8},{8,16},{16,24},{1,9},{9,17},{17,25},{2,10},{10,18},{18,26},{... | collective-permute-start | bytes 24584 | tf_op jit(solution)/shard_map/ppermute | solution.py:22
  13.9 5.5 collective-permute-start.1
  19.5 12.8 %collective-permute-start.2 = (f32[6,1,128]{2,1,0:T(1,128)S(1)}, f32[6,1,128]{2,1,0:T(1,128)S(1)}, u32[]{:S(2)}, u32[]{:S(2)}) collective-permute-start(f32[6,1,128]{2,1,0:T(1,128)S(1)} %get-tuple-element.1763), channel_id=1, source_target_pairs={{0,2},{2,4},{4,6},{1,3},{3,5},{5,7},{8,10},{10,12},{12,14},{9,11},... | collective-permute-start | bytes 9224 | tf_op jit(solution)/shard_map/ppermute | solution.py:22
  22.9 9.4 %collective-permute-start.3 = (f32[6,1,128]{2,1,0:T(1,128)S(1)}, f32[6,1,128]{2,1,0:T(1,128)S(1)}, u32[]{:S(2)}, u32[]{:S(2)}) collective-permute-start(f32[6,1,128]{2,1,0:T(1,128)S(1)} %get-tuple-element.1764), channel_id=1, source_target_pairs={{2,0},{4,2},{6,4},{3,1},{5,3},{7,5},{10,8},{12,10},{14,12},{11,9},... | collective-permute-start | bytes 9224 | tf_op jit(solution)/shard_map/ppermute | solution.py:23
  32.4 5.3 collective-permute-start.4
  33.7 4.0 collective-permute-start.5
  37.9 8.1 collective-permute-start.8
  42.5 9.0 collective-permute-start.9
  58.2 8.5 collective-permute-start.10
  63.9 5.9 collective-permute-start.11
  269.5 5.4 collective-permute-start.12
  273.1 5.6 collective-permute-start.13
  278.7 5.5 collective-permute-start.14
  282.9 5.5 collective-permute-start.15
  288.6 3.9 collective-permute-start.16
  343.3 5.6 collective-permute-start.19
  348.9 6.2 collective-permute-start.20
  353.1 5.5 collective-permute-start.21
  409.6 5.1 collective-permute-start.24
  412.9 5.6 collective-permute-start.25
  418.5 5.5 collective-permute-start.26
  422.7 5.5 collective-permute-start.27
  478.7 4.6 collective-permute-start.30
  481.8 5.6 collective-permute-start.31
  487.5 9.5 %collective-permute-start.32 = (f32[2,6,1,128]{3,2,1,0:T(1,128)S(1)}, f32[2,6,1,128]{3,2,1,0:T(1,128)S(1)}, u32[]{:S(2)}, u32[]{:S(2)}) collective-permute-start(f32[2,6,1,128]{3,2,1,0:T(1,128)S(1)} %get-tuple-element.1737), channel_id=1, source_target_pairs={{0,2},{2,4},{4,6},{1,3},{3,5},{5,7},{8,10},{10,12},{12,14},{9,11},... | collective-permute-start | bytes 18440 | tf_op jit(solution)/shard_map/ppermute | solution.py:22
  491.7 5.5 collective-permute-start.33
  549.6 6.0 collective-permute-start.36
  552.9 5.6 collective-permute-start.37
  558.5 9.1 %collective-permute-start.38 = (f32[2,6,1,128]{3,2,1,0:T(1,128)S(1)}, f32[2,6,1,128]{3,2,1,0:T(1,128)S(1)}, u32[]{:S(2)}, u32[]{:S(2)}) collective-permute-start(f32[2,6,1,128]{3,2,1,0:T(1,128)S(1)} %get-tuple-element.1735), channel_id=1, source_target_pairs={{0,2},{2,4},{4,6},{1,3},{3,5},{5,7},{8,10},{10,12},{12,14},{9,11},... | collective-permute-start | bytes 18440 | tf_op jit(solution)/shard_map/ppermute | solution.py:22
  562.7 5.5 collective-permute-start.39
  619.1 8.0 collective-permute-start.42
  622.3 5.6 collective-permute-start.43
  628.0 6.1 collective-permute-start.44
  632.2 5.5 collective-permute-start.45
  637.8 6.3 collective-permute-start.46
  639.1 5.0 collective-permute-start.47
  691.9 4.6 collective-permute-start.48
  694.6 5.6 collective-permute-start.49
  700.2 9.1 %collective-permute-start.50 = (f32[2,6,1,128]{3,2,1,0:T(1,128)S(1)}, f32[2,6,1,128]{3,2,1,0:T(1,128)S(1)}, u32[]{:S(2)}, u32[]{:S(2)}) collective-permute-start(f32[2,6,1,128]{3,2,1,0:T(1,128)S(1)} %get-tuple-element.1731), channel_id=1, source_target_pairs={{0,2},{2,4},{4,6},{1,3},{3,5},{5,7},{8,10},{10,12},{12,14},{9,11},... | collective-permute-start | bytes 18440 | tf_op jit(solution)/shard_map/ppermute | solution.py:22
  704.4 5.5 collective-permute-start.51
  761.6 7.4 collective-permute-start.54
  764.1 5.6 collective-permute-start.55
  769.8 6.1 collective-permute-start.56
  774.0 5.5 collective-permute-start.57
  779.6 6.5 collective-permute-start.58
  780.9 5.2 collective-permute-start.59
  (46 other events, 2008.0 us)
where the time goes:
time: 925 us; the launch traced here: 912 us
  blocking collectives  446 us (48%)
  starting transfers between devices  128 us (14%)
  other arithmetic  98.5 us (11%)
  between operations  91.4 us (10%)
  local copies, waits for them, and re-layouts  68.3 us (7%)
  waiting for transfers between devices  58.4 us (6%)
  matrix products  21.4 us (2%)
    psum x8, blocking collectives, body(): lax.psum((jnp.dot(basis_c, vector_new, precision=highest), jnp.dot(known_...  324 us
    ppermute x30, starting transfers between devices, padded_2(): before = lax.ppermute(last, axis, up)  89.4 us
    ppermute x30, waiting for transfers between devices, padded_2(): after = lax.ppermute(leading, axis, down)  56.5 us
    another operation x61, other arithmetic  46.9 us
    psum x1, blocking collectives, body(): lax.psum(jnp.dot(flat_images, flat_images.T, precision=highest), ('px', '...  42.2 us
    psum x1, blocking collectives, body(): lax.psum(jnp.dot(residual, residual, precision=highest), ('px', 'py', 'pz'))  40.2 us
    psum x1, blocking collectives, body(): lax.psum(jnp.dot(basis_c, first_residual, precision=highest), ('px', 'py'...  39.8 us
    ppermute x30, starting transfers between devices, padded_2(): after = lax.ppermute(leading, axis, down)  38.8 us
  transfers between devices with their start and end apart: 60, of which 27 were waited for; matrix products, arithmetic and copies ran while one was open for 7% of the time, Pallas kernels for 0%

commit v1 on v0

v1 whole, which is shorter than its diff:
```python
import functools
import itertools

import jax
import jax.numpy as jnp
from jax import lax
from jax.experimental import pallas as pl
from jax.experimental.pallas import tpu as pltpu
from jax.sharding import PartitionSpec as P

STEPS = 8
MESH = pl.DeviceIdType.MESH
AXES = ("px", "py", "pz")
GROUPS = (("py", "pz"), ("px",))

edge_weight = 0.25 ** (1.0 / 3.0)
middle_weight = 2.0 * edge_weight
shift_value = 0.4

DIRS = [d for d in itertools.product((-1, 0, 1), repeat=3) if d != (0, 0, 0)]


def kernel(
    sizes,
    rhs, guess, cond, rec,
    sol_out, res_out, hes_out,
    src, img, bface, bedge, pack, pface, pedge,
    bx, by, bc,
    zm, zx, zy, zc,
    mx, my, mc,
    wbuf, wface, wedge,
    fields, kext, diag, temp, zext,
    gpart, gred1, gred2, sred1, sred2,
    mat, hcols, scale, coef, ecoef,
    hsend, hrecv, rsend, rrecv,
):
    nsz = dict(zip(AXES, sizes))
    me = {a: lax.axis_index(a) for a in AXES}
    K, X, Y, Z = rec.shape
    NF = K + 2
    C0 = K
    f32 = jnp.float32
    lane3 = lax.broadcasted_iota(jnp.int32, (X + 2, Y + 8, Z), 2)
    lane2 = lax.broadcasted_iota(jnp.int32, (32, Z), 1)
    row2 = lax.broadcasted_iota(jnp.int32, (32, Z), 0)

    def exists(d):
        ok = None
        for a, s in zip(AXES, d):
            if s == 0:
                continue
            here = (me[a] < nsz[a] - 1) if s > 0 else (me[a] > 0)
            ok = here if ok is None else jnp.logical_and(ok, here)
        return ok

    def possible(d):
        return all(s == 0 or nsz[a] > 1 for a, s in zip(AXES, d))

    dirs = [(i, d) for i, d in enumerate(DIRS) if possible(d)]

    def target(d):
        return tuple(me[a] + s for a, s in zip(AXES, d))

    def group_info(g):
        n = 1
        rank = 0
        for a in GROUPS[g]:
            n *= nsz[a]
            rank = rank * nsz[a] + me[a]
        return n, rank

    def member(g, r):
        co = dict(me)
        for a in reversed(GROUPS[g]):
            co[a] = lax.rem(r, nsz[a])
            r = lax.div(r, nsz[a])
        return tuple(co[a] for a in AXES)

    def copies(sends, recvs, slot):
        out = []
        for i, (dx, dy, dz) in dirs:
            main, face, edge = sends(dz)
            rm, rx, ry, rc = recvs(-dz)
            hx, hy = int(dx > 0), int(dy > 0)
            if dx == 0 and dy == 0:
                s, t = main, rm
            elif dy == 0:
                s, t = main.at[:, X - 1 if hx else 0], rx.at[1 - hx]
            elif dx == 0:
                s, t = face.at[hy], ry.at[1 - hy]
            else:
                s, t = edge.at[hx, hy], rc.at[1 - hx, 1 - hy]
            d = (dx, dy, dz)
            out.append((d, pltpu.make_async_remote_copy(
                src_ref=s, dst_ref=t,
                send_sem=hsend.at[slot, i], recv_sem=hrecv.at[slot, i],
                device_id=target(d), device_id_type=MESH,
            )))
        return out

    def start_halo(cs):
        for d, c in cs:
            pl.when(exists(d))(c.start)

    def wait_recv(cs):
        for d, c in cs:
            pl.when(exists(tuple(-s for s in d)))(c.wait_recv)

    def wait_send(cs):
        for d, c in cs:
            pl.when(exists(d))(c.wait_send)

    def batch_copies(b):
        def sends(dz):
            if dz == 0:
                return (src if b == 0 else img), bface.at[b], bedge.at[b]
            h = int(dz > 0)
            return pack.at[b, h], pface.at[b, h], pedge.at[b, h]

        def recvs(z):
            if z == 0:
                return None, bx.at[b], by.at[b], bc.at[b]
            h = int(z > 0)
            return zm.at[b, h], zx.at[b, h], zy.at[b, h], zc.at[b, h]

        return copies(sends, recvs, b)

    def step_copies(par):
        def sends(dz):
            return wbuf.at[par], wface.at[par], wedge.at[par]

        def recvs(z):
            if z == 0:
                return None, mx.at[par], my.at[par], mc.at[par]
            h = int(z > 0)
            return zm.at[2 + par, h], zx.at[2 + par, h], zy.at[2 + par, h], zc.at[2 + par, h]

        return copies(sends, recvs, 2 + par)

    def pack_faces(val, face, edge, row, erow):
        for h, y in ((0, 0), (1, Y - 1)):
            for x in range(X):
                face[h, pl.ds(row + x, 1), :] = val[x, y : y + 1, :]
            edge[0, h, pl.ds(erow, 1), :] = val[0, y : y + 1, :]
            edge[1, h, pl.ds(erow, 1), :] = val[X - 1, y : y + 1, :]

    def assemble(dst, main, rx, ry, rc, f, row, erow):
        dst[1 : X + 1, 0:Y, :] = main
        dst[0, 0:Y, :] = rx[0, f]
        dst[X + 1, 0:Y, :] = rx[1, f]
        for h, y in ((1, Y), (0, Y + 7)):
            for x in range(X):
                dst[1 + x, y : y + 1, :] = ry[h, pl.ds(row + x, 1), :]
            dst[0, y : y + 1, :] = rc[0, h, pl.ds(erow, 1), :]
            dst[X + 1, y : y + 1, :] = rc[1, h, pl.ds(erow, 1), :]

    def assemble_zones(slot):
        for h in range(2):
            assemble(zext.at[h], zm[slot, h, 0], zx.at[slot, h], zy.at[slot, h], zc.at[slot, h], 0, 0, 0)

    def zone_field(f):
        low = pltpu.roll(zext[0], lax.rem(2 * Z - 1 - f, Z), 2)
        high = pltpu.roll(zext[1], lax.rem(Z - f, Z), 2)
        return jnp.where(lane3 == Z - 1, low, jnp.where(lane3 == 0, high, 0.0))

    def pack_lanes(get, count, b):
        lane = lax.broadcasted_iota(jnp.int32, (X, Y, Z), 2)
        low = jnp.zeros((X, Y, Z), f32)
        high = jnp.zeros((X, Y, Z), f32)
        for f in range(count):
            v = get(f)
            low = jnp.where(lane == f, pltpu.roll(v, f, 2) if f else v, low)
            high = jnp.where(lane == f, pltpu.roll(v, (f + 1) % Z, 2), high)
        for h, v in ((0, low), (1, high)):
            pack[b, h, 0] = v
            pack_faces(v, pface.at[b, h], pedge.at[b, h], 0, 0)

    def stencil(e, b):
        left = pltpu.roll(jnp.where(lane3 == Z - 1, b, e), 1, 2)
        right = pltpu.roll(jnp.where(lane3 == 0, b, e), Z - 1, 2)
        az = edge_weight * (left + right) + middle_weight * e
        ay = edge_weight * (pltpu.roll(az, 1, 1) + pltpu.roll(az, Y + 7, 1)) + middle_weight * az
        ay = ay[:, :Y]
        ax = edge_weight * (ay[:X] + ay[2:]) + middle_weight * ay[1 : X + 1]
        return ax - 2.0 * e[1 : X + 1, :Y]

    def apply(e, b):
        k = kext[0]
        near = stencil(e, b)
        far = stencil(k * e, kext[1] * b)
        return diag[...] * e[1 : X + 1, :Y] - 0.5 * k[1 : X + 1, :Y] * near - 0.5 * far

    def tile_sum(v):
        v = jnp.sum(v.reshape(X * Y // 8, 8, Z), axis=0)
        return jnp.sum(v, axis=0, keepdims=True)

    def all_reduce(value, bufs, slot):
        total = value
        for g in range(len(GROUPS)):
            n, rank = group_info(g)
            buf = bufs[g]
            buf[rank] = total
            cs = []
            for k in range(1, n):
                c = pltpu.make_async_remote_copy(
                    src_ref=buf.at[rank], dst_ref=buf.at[rank],
                    send_sem=rsend.at[slot, g, k], recv_sem=rrecv.at[slot, g, k],
                    device_id=member(g, lax.rem(rank + k, n)), device_id_type=MESH,
                )
                c.start()
                cs.append((k, c))
            for k, c in cs:
                pltpu.make_async_remote_copy(
                    src_ref=buf.at[rank], dst_ref=buf.at[lax.rem(rank + n - k, n)],
                    send_sem=rsend.at[slot, g, k], recv_sem=rrecv.at[slot, g, k],
                    device_id=member(g, lax.rem(rank + k, n)), device_id_type=MESH,
                ).wait_recv()
            total = buf[0]
            for r in range(1, n):
                total = total + buf[r]
            for k, c in cs:
                c.wait_send()
        return total

    for ref in (bx, by, bc, zm, zx, zy, zc, mx, my, mc, wface, wedge, bface, bedge, pface, pedge):
        lead = ref.shape[0]

        def clear(i, carry, ref=ref):
            ref[i] = jnp.zeros(ref.shape[1:], f32)
            return carry

        lax.fori_loop(0, lead, clear, 0)

    def clear_fields(i, carry):
        fields[i] = jnp.zeros(fields.shape[1:], f32)
        return carry

    lax.fori_loop(0, fields.shape[0], clear_fields, 0)
    kext[...] = jnp.zeros(kext.shape, f32)
    temp[...] = jnp.zeros(temp.shape, f32)
    zext[...] = jnp.zeros(zext.shape, f32)
    img[NF - 1] = jnp.zeros((X, Y, Z), f32)

    def load_field(f, carry):
        v = rec[f]
        src[f] = v
        pack_faces(v, bface.at[0], bedge.at[0], f * X, f)
        return carry

    lax.fori_loop(0, K, load_field, 0)
    for f, ref in ((K, guess), (K + 1, cond)):
        v = ref[...]
        src[f] = v
        pack_faces(v, bface.at[0], bedge.at[0], f * X, f)
    pack_lanes(lambda f: src[f], NF, 0)

    barrier = pltpu.get_barrier_semaphore()
    count = jnp.int32(0)
    for _, d in dirs:
        ok = exists(d)

        @pl.when(ok)
        def _(d=d):
            pl.semaphore_signal(barrier, inc=1, device_id=target(d), device_id_type=MESH)

        count = count + ok.astype(jnp.int32)
    for g in range(len(GROUPS)):
        n, rank = group_info(g)
        for k in range(1, n):
            pl.semaphore_signal(
                barrier, inc=1, device_id=member(g, lax.rem(rank + k, n)), device_id_type=MESH
            )
        count = count + (n - 1)
    pl.semaphore_wait(barrier, count)

    first = batch_copies(0)
    start_halo(first)
    wait_recv(first)
    assemble_zones(0)
    assemble(kext.at[0], src[K + 1], bx.at[0], by.at[0], bc.at[0], K + 1, (K + 1) * X, K + 1)
    kext[1] = zone_field(K + 1)
    k_all = kext[0]
    diag[...] = shift_value + 7.0 * k_all[1 : X + 1, :Y] + 0.5 * stencil(k_all, kext[1])

    def image(f, carry):
        assemble(temp, src[f], bx.at[0], by.at[0], bc.at[0], f, f * X, f)
        v = apply(temp[...], zone_field(f))
        img[f] = v
        return carry

    lax.fori_loop(0, K + 1, image, 0)
    img[K] = rhs[...] - img[K]

    def face_image(f, carry):
        pack_faces(img[f], bface.at[1], bedge.at[1], f * X, f)
        return carry

    lax.fori_loop(0, K + 1, face_image, 0)
    pack_lanes(lambda f: img[f], K + 1, 1)
    second = batch_copies(1)
    start_halo(second)

    GR = gpart.shape[1]

    def gram_part(a, carry):
        va = img[a]
        rows = [tile_sum(img[b] * va) for b in range(K + 1)]
        rows.append(jnp.zeros((GR - K - 1, Z), f32))
        gpart[a] = jnp.concatenate(rows, axis=0)
        return carry

    lax.fori_loop(0, K + 1, gram_part, 0)
    lane_g = lax.broadcasted_iota(jnp.int32, (GR, Z), 1)
    gram = jnp.zeros((GR, Z), f32)
    for a in range(K + 1):
        gram = jnp.where(lane_g == a, jnp.sum(gpart[a], axis=1, keepdims=True), gram)
    gram = all_reduce(gram, (gred1, gred2), 2)

    lane_k = lax.broadcasted_iota(jnp.int32, (K, Z), 1)
    row_k = lax.broadcasted_iota(jnp.int32, (K, Z), 0)
    a_mat = jnp.where(lane_k < K, gram[:K], 0.0)
    for k in range(K):
        prow = a_mat[k : k + 1, :]
        pcol = a_mat[:, k : k + 1]
        inv_p = 1.0 / a_mat[k : k + 1, k : k + 1]
        prow_s = jnp.where(lax.broadcasted_iota(jnp.int32, (1, Z), 1) == k, 1.0, prow) * inv_p
        base = jnp.where(lane_k == k, 0.0, a_mat)
        a_mat = jnp.where(row_k == k, jnp.broadcast_to(prow_s, (K, Z)), base - pcol * prow_s)
    mat[...] = jnp.where(lane2 == row2, 1.0, 0.0)
    mat[0:K, :] = a_mat
    grow = jnp.where(lax.broadcasted_iota(jnp.int32, (1, Z), 1) < K, gram[K : K + 1, :], 0.0)
    ecoef[...] = jnp.broadcast_to(jnp.sum(a_mat * grow, axis=1, keepdims=True), (K, Z))

    wait_recv(second)
    assemble_zones(1)

    def extend(f, carry):
        assemble(fields.at[f, 0], img[f], bx.at[1], by.at[1], bc.at[1], f, f * X, f)
        fields[f, 1] = zone_field(f)
        return carry

    lax.fori_loop(0, K + 1, extend, 0)

    def begin(p, carry):
        z, x = lax.div(p, X + 2), lax.rem(p, X + 2)
        v = fields[C0, z, x]
        for a in range(K):
            v = v - ecoef[a : a + 1, :] * fields[a, z, x]
        fields[C0, z, x] = v
        return carry

    lax.fori_loop(0, 2 * (X + 2), begin, 0)
    wait_send(first)
    wait_send(second)
    hcols[...] = jnp.zeros((32, Z), f32)
    scale[...] = jnp.where(row2 < K, 1.0, 0.0)

    def step(j, carry):
        par = lax.rem(j, 2)
        u = fields[C0 + j, 0]
        w = apply(u, fields[C0 + j, 1])
        wbuf[par, 0] = w
        pack_faces(w, wface.at[par], wedge.at[par], 0, 0)
        cs = step_copies(par)

        @pl.when(j < STEPS - 1)
        def _():
            start_halo(cs)

        rows = [tile_sum(fields[f, 0, 1 : X + 1, 0:Y, :] * w) for f in range(K + STEPS)]
        ui = u[1 : X + 1, :Y]
        rows.append(tile_sum(w * w))
        rows.append(tile_sum(ui * ui))
        rows.append(jnp.zeros((32 - K - STEPS - 2, Z), f32))
        sums = jnp.sum(jnp.concatenate(rows, axis=0), axis=1, keepdims=True)
        part = jnp.sum(jnp.where(lane2 == row2, sums, 0.0), axis=0, keepdims=True)
        total = all_reduce(jnp.broadcast_to(part, (8, Z)), (sred1.at[par], sred2.at[par]), par)
        total = jnp.concatenate([total] * 4, axis=0)
        c = jnp.broadcast_to(jnp.sum(mat[...] * total, axis=1, keepdims=True), (32, Z))
        uu = c[K + STEPS + 1 : K + STEPS + 2, :]
        sc = jnp.where(row2 == C0 + j, 1.0 / uu, scale[...])
        scale[...] = sc
        hcols[...] = jnp.where(lane2 == j, c, hcols[...])
        inv_n = 1.0 / jnp.sqrt(uu)
        coef[...] = jnp.where(
            row2 < K + STEPS, c * sc * inv_n, jnp.where(row2 == 30, inv_n, total)
        )

        @pl.when(j < STEPS - 1)
        def _():
            wait_recv(cs)
            slot = 2 + par
            assemble(temp, wbuf[par, 0], mx.at[par], my.at[par], mc.at[par], 0, 0, 0)
            fields[C0 + 1 + j, 0] = temp[...]
            assemble_zones(slot)
            fields[C0 + 1 + j, 1] = jnp.where(
                lane3 == Z - 1, zext[0], jnp.where(lane3 == 0, zext[1], 0.0)
            )

        @pl.when(j == STEPS - 1)
        def _():
            fields[C0 + STEPS, 0, 1 : X + 1, 0:Y, :] = wbuf[par, 0]

        def update(p, carry):
            z, x = lax.div(p, X + 2), lax.rem(p, X + 2)
            v = coef[30:31, :] * fields[C0 + 1 + j, z, x]
            v2 = jnp.zeros_like(v)
            for a in range(0, K + STEPS, 2):
                v = v - coef[a : a + 1, :] * fields[a, z, x]
                v2 = v2 - coef[a + 1 : a + 2, :] * fields[a + 1, z, x]
            fields[C0 + 1 + j, z, x] = v + v2
            return carry

        lax.fori_loop(0, 2 * (X + 2), update, 0)

        @pl.when(j < STEPS - 1)
        def _():
            wait_send(cs)

        return carry

    lax.fori_loop(0, STEPS, step, 0)

    lane8 = lane2[:8]
    row8 = row2[:8]
    hc = hcols[...]
    inv_n2 = scale[C0 : C0 + STEPS, :]
    inv_col = jnp.sqrt(inv_n2)
    n_col = 1.0 / inv_col
    inv_row = jnp.sum(jnp.where(lane8 == row8, inv_col, 0.0), axis=0, keepdims=True)
    last_c = jnp.sum(jnp.where(lane2 == STEPS - 1, hc, 0.0), axis=1, keepdims=True)
    raw = jnp.broadcast_to(coef[31:32, :], (32, Z))
    raw_col = jnp.sum(jnp.where(lane2 == row2, raw, 0.0), axis=1, keepdims=True)
    terms = jnp.where(row2[:, :1] < K + STEPS, raw_col * last_c * scale[:, :1], 0.0)
    used = jnp.sum(terms, axis=0, keepdims=True)
    last_sq = (raw_col[K + STEPS : K + STEPS + 1] - used) * inv_n2[STEPS - 1 : STEPS, :1]
    last_n = jnp.sqrt(last_sq)
    upper = hc[C0 : C0 + STEPS] * inv_col * inv_row
    upper = jnp.where(lane8 < STEPS, upper, 0.0)
    upper = jnp.where(lane8 == row8 - 1, n_col, upper)
    lane1 = lane2[:1]
    bottom = jnp.where(lane1 == STEPS - 1, last_n, 0.0)
    hes = jnp.concatenate([upper, bottom], axis=0)
    hes_out[...] = hes[:, :STEPS]

    rows = [hes[i : i + 1] for i in range(STEPS + 1)]
    rows[0] = jnp.where(lane1 == STEPS, n_col[0:1], rows[0])
    for i in range(STEPS):
        top, low = rows[i][:, i : i + 1], rows[i + 1][:, i : i + 1]
        inv_r = 1.0 / jnp.sqrt(top * top + low * low)
        cs_, sn = top * inv_r, low * inv_r
        rows[i], rows[i + 1] = cs_ * rows[i] + sn * rows[i + 1], cs_ * rows[i + 1] - sn * rows[i]
    ysol = jnp.zeros((1, Z), f32)
    for i in range(STEPS - 1, -1, -1):
        known = jnp.sum(jnp.where(lane1 > i, rows[i] * ysol, 0.0), axis=1, keepdims=True)
        yi = (rows[i][:, STEPS : STEPS + 1] - known) / rows[i][:, i : i + 1]
        ysol = jnp.where(lane1 == i, yi, ysol)

    rcoef = ecoef[:, :1] - jnp.sum(hc[:K] * (ysol * inv_row), axis=1, keepdims=True)
    ycol = jnp.sum(jnp.where(lane8 == row8, ysol * inv_row, 0.0), axis=1, keepdims=True)
    hy8 = jnp.sum(upper * ysol, axis=1, keepdims=True) * inv_col[:, :1]
    hy9 = jnp.sum(bottom * ysol, axis=1, keepdims=True) / last_n
    out = guess[...]
    for a in range(K):
        out = out + rcoef[a : a + 1, :] * rec[a]
    res = fields[C0, 0, 1 : X + 1, 0:Y, :]
    for i in range(STEPS):
        ui = fields[C0 + i, 0, 1 : X + 1, 0:Y, :]
        out = out + ycol[i : i + 1, :] * ui
        res = res - hy8[i : i + 1, :] * ui
    res = res - hy9 * fields[C0 + STEPS, 0, 1 : X + 1, 0:Y, :]
    sol_out[...] = out
    res_out[...] = res


def round_up(n, m):
    return (n + m - 1) // m * m


def solution(mesh):
    sizes = tuple(mesh.shape[a] for a in AXES)

    def body(right_side, start_guess, conductivity, recycled):
        K, X, Y, Z = recycled.shape
        NF = K + 2
        FR, ER, XR = round_up(NF * X, 8), round_up(NF, 8), round_up(X, 8)
        groups = []
        for g in GROUPS:
            n = 1
            for a in g:
                n *= mesh.shape[a]
            groups.append(n)
        biggest = max(groups)
        GR = round_up(K + 1, 8)
        V = lambda *s: pltpu.VMEM(s, jnp.float32)
        vm = pl.BlockSpec(memory_space=pltpu.VMEM)
        shape = jax.ShapeDtypeStruct((X, Y, Z), jnp.float32)
        return pl.pallas_call(
            functools.partial(kernel, sizes),
            out_shape=(shape, shape, jax.ShapeDtypeStruct((STEPS + 1, STEPS), jnp.float32)),
            in_specs=[vm] * 4,
            out_specs=(vm, vm, vm),
            scratch_shapes=[
                V(NF, X, Y, Z), V(NF, X, Y, Z),
                V(2, 2, FR, Z), V(2, 2, 2, ER, Z),
                V(2, 2, 1, X, Y, Z), V(2, 2, 2, XR, Z), V(2, 2, 2, 2, 8, Z),
                V(2, 2, NF, Y, Z), V(2, 2, FR, Z), V(2, 2, 2, ER, Z),
                V(4, 2, 1, X, Y, Z), V(4, 2, 2, 1, Y, Z), V(4, 2, 2, XR, Z), V(4, 2, 2, 2, 8, Z),
                V(2, 2, 1, Y, Z), V(2, 2, XR, Z), V(2, 2, 2, 8, Z),
                V(2, 1, X, Y, Z), V(2, 2, XR, Z), V(2, 2, 2, 8, Z),
                V(K + STEPS + 1, 2, X + 2, Y + 8, Z), V(2, X + 2, Y + 8, Z), V(X, Y, Z),
                V(X + 2, Y + 8, Z), V(2, X + 2, Y + 8, Z),
                V(K + 1, GR, Z), V(groups[0], GR, Z), V(groups[1], GR, Z),
                V(2, groups[0], 8, Z), V(2, groups[1], 8, Z),
                V(32, Z), V(32, Z), V(32, Z), V(32, Z), V(K, Z),
                pltpu.SemaphoreType.DMA((4, 26)), pltpu.SemaphoreType.DMA((4, 26)),
                pltpu.SemaphoreType.DMA((3, 2, biggest)), pltpu.SemaphoreType.DMA((3, 2, biggest)),
            ],
            compiler_params=pltpu.CompilerParams(collective_id=0, has_side_effects=True),
        )(right_side, start_guess, conductivity, recycled)

    return jax.shard_map(
        body,
        mesh=mesh,
        in_specs=(P(*AXES), P(*AXES), P(*AXES), P(None, *AXES)),
        out_specs=(P(*AXES), P(*AXES), P()),
        check_vma=False,
    )
```

time: 925 us -> 104 us (0.11); the launches traced: 912 us -> 104 us
  blocking collectives: 446 us -> 0 us
  starting transfers between devices: 128 us -> 0 us
  Pallas kernels: 0 us -> 100 us
  other arithmetic: 98.5 us -> 0 us
  between operations: 91.4 us -> 0.64 us
  local copies, waits for them, and re-layouts: 68.3 us -> 3.36 us
  waiting for transfers between devices: 58.4 us -> 0 us
  matrix products: 21.4 us -> 0 us
    psum x11 -> x0, blocking collectives: 446 us -> none  [the longest x8 324 us: body(): lax.psum((jnp.dot(basis_c, vector_new, precision=highest), jnp.dot(known_...]
    ppermute x60 -> x0, starting transfers between devices: 128 us -> none  [the longest x30 89.4 us: padded_2(): before = lax.ppermute(last, axis, up)]
    pallas_call x0 -> x1, Pallas kernels: none -> 100 us  [body(): pl.pallas_call(functools.partial(kernel, sizes), out_shape=(shape, shape,...]
    ppermute x60 -> x0, waiting for transfers between devices: 58.4 us -> none  [the longest x30 56.5 us: padded_2(): after = lax.ppermute(leading, axis, down)]
    another operation x61 -> x0, other arithmetic: 46.9 us -> none
    slice x63 -> x0, local copies, waits for them, and re-layouts: 34.9 us -> none  [the longest x16 9.94 us: cholesky_low(): pivot = jnp.sqrt(gram[column, column] - partial_sum[column])]
    dot_general x42 -> x0, matrix products: 21.4 us -> none  [the longest x8 5.81 us: body(): jnp.dot(basis_c, vector_new, precision=highest)]
    scatter x106 -> x0, local copies, waits for them, and re-layouts: 19.1 us -> none  [the longest x8 10.7 us: body(): hessenberg = hessenberg.at[:column + 1, column].set(coeff_v)]
  transfers between devices with their start and end apart: 60 -> 0, of which waited for: 27 -> 0; matrix products, arithmetic and copies ran while one was open for 7% -> 0% of each run, Pallas kernels for 0% -> 0%
where the time goes in v1:
time: 104 us
  Pallas kernels  100 us (96%)
  local copies, waits for them, and re-layouts  3.36 us (3%)
    pallas_call x1, Pallas kernels, body(): pl.pallas_call(functools.partial(kernel, sizes), out_shape=(shape, shape,...  100 us

profile of v1, /device:TPU:0, one launch (start us, length us, event | category | flops | bytes accessed | tf_op | source)
XLA Modules:
  0.0 104.2 jit_solution(18011783837409675829)
XLA Ops:
  0.6 100.2 %shard_map.67 = (f32[4,16,128]{2,1,0:T(8,128)}, f32[4,16,128]{2,1,0:T(8,128)}, f32[9,8]{1,0:T(8,128)}) custom-call(f32[4,16,128]{2,1,0:T(8,128)} %rhs.1, f32[4,16,128]{2,1,0:T(8,128)} %guess.1, f32[4,16,128]{2,1,0:T(8,128)} %cond.1, f32[16,4,16,128]{3,2,1,0:T(8,128)} %rec.1), custom_call_target="tpu_custom_call" | custom-call | tf_op jit(solution)/shard_map/pallas_call | solution.py:498
  100.8 1.4 %copy.7 = f32[9,8]{0,1:T(8,128)} copy(f32[9,8]{1,0:T(8,128)} %get-tuple-element.5) | data formatting | bytes 576 | tf_op jit(solution)/shard_map/pallas_call | solution.py:498
  102.2 0.0 copy-start
  102.2 1.4 %copy.10 = f32[4,16,128]{2,1,0:T(8,128)} copy(f32[4,16,128]{2,1,0:T(8,128)} %get-tuple-element.9) | data formatting | bytes 65536
  103.6 0.0 copy-done
  103.6 0.6 copy.11
Async XLA Ops:
  102.2 1.4 %copy-start = (f32[4,16,128]{2,1,0:T(8,128)S(1)}, f32[4,16,128]{2,1,0:T(8,128)}, u32[]{:S(2)}) copy-start(f32[4,16,128]{2,1,0:T(8,128)} %get-tuple-element.10) | copy-start | bytes 98308

commit v2 on v1

--- a/solution.py
+++ b/solution.py
@@ -11,7 +11,9 @@
 STEPS = 8
 MESH = pl.DeviceIdType.MESH
 AXES = ("px", "py", "pz")
-GROUPS = (("py", "pz"), ("px",))
+TWO = (("py", "pz"), ("px",))
+ONE = (("px", "py", "pz"),)
+CHUNK = 8
 
 edge_weight = 0.25 ** (1.0 / 3.0)
 middle_weight = 2.0 * edge_weight
@@ -21,7 +23,7 @@
 
 
 def kernel(
-    sizes,
+    sizes, groups,
     rhs, guess, cond, rec,
     sol_out, res_out, hes_out,
     src, img, bface, bedge, pack, pface, pedge,
@@ -61,24 +63,26 @@
     def target(d):
         return tuple(me[a] + s for a, s in zip(AXES, d))
 
-    def group_info(g):
+    def group_info(group):
         n = 1
         rank = 0
-        for a in GROUPS[g]:
+        for a in group:
             n *= nsz[a]
             rank = rank * nsz[a] + me[a]
         return n, rank
 
-    def member(g, r):
+    def member(group, r):
         co = dict(me)
-        for a in reversed(GROUPS[g]):
+        for a in reversed(group):
             co[a] = lax.rem(r, nsz[a])
             r = lax.div(r, nsz[a])
         return tuple(co[a] for a in AXES)
 
-    def copies(sends, recvs, slot):
+    def copies(sends, recvs, slot, zones):
         out = []
         for i, (dx, dy, dz) in dirs:
+            if (dz != 0) not in zones:
+                continue
             main, face, edge = sends(dz)
             rm, rx, ry, rc = recvs(-dz)
             hx, hy = int(dx > 0), int(dy > 0)
@@ -110,20 +114,27 @@
         for d, c in cs:
             pl.when(exists(d))(c.wait_send)
 
-    def batch_copies(b):
+    NC = (NF + CHUNK - 1) // CHUNK
+
+    def batch_copies(b, c):
+        f0, f1 = c * CHUNK, min((c + 1) * CHUNK, NF)
+        fs, es = pl.ds(f0, f1 - f0), pl.ds(f0, CHUNK)
+        rows = pl.ds(f0 * X, min(CHUNK * X, bface.shape[2] - f0 * X))
+
         def sends(dz):
             if dz == 0:
-                return (src if b == 0 else img), bface.at[b], bedge.at[b]
+                body = (src if b == 0 else img).at[fs]
+                return body, bface.at[b, :, rows], bedge.at[b, :, :, es]
             h = int(dz > 0)
             return pack.at[b, h], pface.at[b, h], pedge.at[b, h]
 
         def recvs(z):
             if z == 0:
-                return None, bx.at[b], by.at[b], bc.at[b]
+                return None, bx.at[b, :, fs], by.at[b, :, rows], bc.at[b, :, :, es]
             h = int(z > 0)
             return zm.at[b, h], zx.at[b, h], zy.at[b, h], zc.at[b, h]
 
-        return copies(sends, recvs, b)
+        return copies(sends, recvs, b * (NC + 1) + c, (c == NC,))
 
     def step_copies(par):
         def sends(dz):
@@ -135,7 +146,7 @@
             h = int(z > 0)
             return zm.at[2 + par, h], zx.at[2 + par, h], zy.at[2 + par, h], zc.at[2 + par, h]
 
-        return copies(sends, recvs, 2 + par)
+        return copies(sends, recvs, 2 * (NC + 1) + par, (False, True))
 
     def pack_faces(val, face, edge, row, erow):
         for h, y in ((0, 0), (1, Y - 1)):
@@ -194,10 +205,10 @@
         v = jnp.sum(v.reshape(X * Y // 8, 8, Z), axis=0)
         return jnp.sum(v, axis=0, keepdims=True)
 
-    def all_reduce(value, bufs, slot):
+    def all_reduce(value, groups, bufs, slot, between):
         total = value
-        for g in range(len(GROUPS)):
-            n, rank = group_info(g)
+        for g, group in enumerate(groups):
+            n, rank = group_info(group)
             buf = bufs[g]
             buf[rank] = total
             cs = []
@@ -205,15 +216,17 @@
                 c = pltpu.make_async_remote_copy(
                     src_ref=buf.at[rank], dst_ref=buf.at[rank],
                     send_sem=rsend.at[slot, g, k], recv_sem=rrecv.at[slot, g, k],
-                    device_id=member(g, lax.rem(rank + k, n)), device_id_type=MESH,
+                    device_id=member(group, lax.rem(rank + k, n)), device_id_type=MESH,
                 )
                 c.start()
                 cs.append((k, c))
+            if g == len(groups) - 1:
+                between()
             for k, c in cs:
                 pltpu.make_async_remote_copy(
                     src_ref=buf.at[rank], dst_ref=buf.at[lax.rem(rank + n - k, n)],
                     send_sem=rsend.at[slot, g, k], recv_sem=rrecv.at[slot, g, k],
-                    device_id=member(g, lax.rem(rank + k, n)), device_id_type=MESH,
+                    device_id=member(group, lax.rem(rank + k, n)), device_id_type=MESH,
                 ).wait_recv()
             total = buf[0]
             for r in range(1, n):
@@ -222,24 +235,34 @@
                 c.wait_send()
         return total
 
-    for ref in (bx, by, bc, zm, zx, zy, zc, mx, my, mc, wface, wedge, bface, bedge, pface, pedge):
-        lead = ref.shape[0]
-
-        def clear(i, carry, ref=ref):
-            ref[i] = jnp.zeros(ref.shape[1:], f32)
-            return carry
-
-        lax.fori_loop(0, lead, clear, 0)
-
-    def clear_fields(i, carry):
-        fields[i] = jnp.zeros(fields.shape[1:], f32)
-        return carry
-
-    lax.fori_loop(0, fields.shape[0], clear_fields, 0)
-    kext[...] = jnp.zeros(kext.shape, f32)
-    temp[...] = jnp.zeros(temp.shape, f32)
-    zext[...] = jnp.zeros(zext.shape, f32)
-    img[NF - 1] = jnp.zeros((X, Y, Z), f32)
+    def clear_all(refs):
+        for ref in refs:
+            def clear(i, carry, ref=ref):
+                ref[i] = jnp.zeros(ref.shape[1:], f32)
+                return carry
+
+            lax.fori_loop(0, ref.shape[0], clear, 0)
+
+    clear_all((bx, by, bc, zm, zx, zy, zc, mx, my, mc))
+    barrier = pltpu.get_barrier_semaphore()
+    count = jnp.int32(0)
+    for _, d in dirs:
+        ok = exists(d)
+
+        @pl.when(ok)
+        def _(d=d):
+            pl.semaphore_signal(barrier, inc=1, device_id=target(d), device_id_type=MESH)
+
+        count = count + ok.astype(jnp.int32)
+    for group in sorted(set(TWO + groups)):
+        n, rank = group_info(group)
+        for k in range(1, n):
+            pl.semaphore_signal(
+                barrier, inc=1, device_id=member(group, lax.rem(rank + k, n)), device_id_type=MESH
+            )
+        count = count + (n - 1)
+
+    clear_all((wface, wedge, bface, bedge, pface, pedge))
 
     def load_field(f, carry):
         v = rec[f]
@@ -253,54 +276,46 @@
         src[f] = v
         pack_faces(v, bface.at[0], bedge.at[0], f * X, f)
     pack_lanes(lambda f: src[f], NF, 0)
-
-    barrier = pltpu.get_barrier_semaphore()
-    count = jnp.int32(0)
-    for _, d in dirs:
-        ok = exists(d)
-
-        @pl.when(ok)
-        def _(d=d):
-            pl.semaphore_signal(barrier, inc=1, device_id=target(d), device_id_type=MESH)
-
-        count = count + ok.astype(jnp.int32)
-    for g in range(len(GROUPS)):
-        n, rank = group_info(g)
-        for k in range(1, n):
-            pl.semaphore_signal(
-                barrier, inc=1, device_id=member(g, lax.rem(rank + k, n)), device_id_type=MESH
-            )
-        count = count + (n - 1)
     pl.semaphore_wait(barrier, count)
 
-    first = batch_copies(0)
-    start_halo(first)
-    wait_recv(first)
+    first = [batch_copies(0, c) for c in range(NC + 1)]
+    second = [batch_copies(1, c) for c in range(NC + 1)]
+    order = [NC - 1] + list(range(NC - 1))
+    for c in [NC] + order:
+        start_halo(first[c])
+    clear_all((fields, kext, zext))
+    temp[...] = jnp.zeros(temp.shape, f32)
+    img[NF - 1] = jnp.zeros((X, Y, Z), f32)
+    wait_recv(first[NC])
     assemble_zones(0)
-    assemble(kext.at[0], src[K + 1], bx.at[0], by.at[0], bc.at[0], K + 1, (K + 1) * X, K + 1)
-    kext[1] = zone_field(K + 1)
-    k_all = kext[0]
-    diag[...] = shift_value + 7.0 * k_all[1 : X + 1, :Y] + 0.5 * stencil(k_all, kext[1])
 
     def image(f, carry):
         assemble(temp, src[f], bx.at[0], by.at[0], bc.at[0], f, f * X, f)
         v = apply(temp[...], zone_field(f))
         img[f] = v
+        pack_faces(v, bface.at[1], bedge.at[1], f * X, f)
         return carry
 
-    lax.fori_loop(0, K + 1, image, 0)
-    img[K] = rhs[...] - img[K]
-
-    def face_image(f, carry):
-        pack_faces(img[f], bface.at[1], bedge.at[1], f * X, f)
-        return carry
-
-    lax.fori_loop(0, K + 1, face_image, 0)
+    for c in order:
+        wait_recv(first[c])
+        if c == NC - 1:
+            assemble(kext.at[0], src[K + 1], bx.at[0], by.at[0], bc.at[0], K + 1, (K + 1) * X, K + 1)
+            kext[1] = zone_field(K + 1)
+            k_all = kext[0]
+            diag[...] = shift_value + 7.0 * k_all[1 : X + 1, :Y] + 0.5 * stencil(k_all, kext[1])
+            lax.fori_loop(c * CHUNK, K + 1, image, 0)
+            v = rhs[...] - img[K]
+            img[K] = v
+            pack_faces(v, bface.at[1], bedge.at[1], K * X, K)
+        else:
+            lax.fori_loop(c * CHUNK, (c + 1) * CHUNK, image, 0)
+        start_halo(second[c])
     pack_lanes(lambda f: img[f], K + 1, 1)
-    second = batch_copies(1)
-    start_halo(second)
+    start_halo(second[NC])
 
     GR = gpart.shape[1]
+    GW = Z // (GR // 8)
+    assert K + 1 <= GW
 
     def gram_part(a, carry):
         va = img[a]
@@ -314,7 +329,24 @@
     gram = jnp.zeros((GR, Z), f32)
     for a in range(K + 1):
         gram = jnp.where(lane_g == a, jnp.sum(gpart[a], axis=1, keepdims=True), gram)
-    gram = all_reduce(gram, (gred1, gred2), 2)
+    def extend_all():
+        for c in second:
+            wait_recv(c)
+        assemble_zones(1)
+
+        def extend(f, carry):
+            assemble(fields.at[f, 0], img[f], bx.at[1], by.at[1], bc.at[1], f, f * X, f)
+            fields[f, 1] = zone_field(f)
+            return carry
+
+        lax.fori_loop(0, K + 1, extend, 0)
+
+    part = gram[:8]
+    for q in range(1, GR // 8):
+        part = part + pltpu.roll(gram[8 * q : 8 * q + 8], q * GW, 1)
+    part = all_reduce(part, TWO, (gred1, gred2), 2, extend_all)
+    gram = [part] + [pltpu.roll(part, Z - q * GW, 1) for q in range(1, GR // 8)]
+    gram = jnp.concatenate(gram, axis=0)
 
     lane_k = lax.broadcasted_iota(jnp.int32, (K, Z), 1)
     row_k = lax.broadcasted_iota(jnp.int32, (K, Z), 0)
@@ -331,16 +363,6 @@
     grow = jnp.where(lax.broadcasted_iota(jnp.int32, (1, Z), 1) < K, gram[K : K + 1, :], 0.0)
     ecoef[...] = jnp.broadcast_to(jnp.sum(a_mat * grow, axis=1, keepdims=True), (K, Z))
 
-    wait_recv(second)
-    assemble_zones(1)
-
-    def extend(f, carry):
-        assemble(fields.at[f, 0], img[f], bx.at[1], by.at[1], bc.at[1], f, f * X, f)
-        fields[f, 1] = zone_field(f)
-        return carry
-
-    lax.fori_loop(0, K + 1, extend, 0)
-
     def begin(p, carry):
         z, x = lax.div(p, X + 2), lax.rem(p, X + 2)
         v = fields[C0, z, x]
@@ -350,8 +372,8 @@
         return carry
 
     lax.fori_loop(0, 2 * (X + 2), begin, 0)
-    wait_send(first)
-    wait_send(second)
+    for c in first + second:
+        wait_send(c)
     hcols[...] = jnp.zeros((32, Z), f32)
     scale[...] = jnp.where(row2 < K, 1.0, 0.0)
 
@@ -374,8 +396,23 @@
         rows.append(jnp.zeros((32 - K - STEPS - 2, Z), f32))
         sums = jnp.sum(jnp.concatenate(rows, axis=0), axis=1, keepdims=True)
         part = jnp.sum(jnp.where(lane2 == row2, sums, 0.0), axis=0, keepdims=True)
-        total = all_reduce(jnp.broadcast_to(part, (8, Z)), (sred1.at[par], sred2.at[par]), par)
-        total = jnp.concatenate([total] * 4, axis=0)
+        def extend_w():
+            @pl.when(j < STEPS - 1)
+            def _():
+                wait_recv(cs)
+                slot = 2 + par
+                assemble(temp, wbuf[par, 0], mx.at[par], my.at[par], mc.at[par], 0, 0, 0)
+                fields[C0 + 1 + j, 0] = temp[...]
+                assemble_zones(slot)
+                fields[C0 + 1 + j, 1] = jnp.where(
+                    lane3 == Z - 1, zext[0], jnp.where(lane3 == 0, zext[1], 0.0)
+                )
+
+            @pl.when(j == STEPS - 1)
+            def _():
+                fields[C0 + STEPS, 0, 1 : X + 1, 0:Y, :] = wbuf[par, 0]
+
+        total = all_reduce(part, groups, (sred1.at[par], sred2.at[par]), par, extend_w)
         c = jnp.broadcast_to(jnp.sum(mat[...] * total, axis=1, keepdims=True), (32, Z))
         uu = c[K + STEPS + 1 : K + STEPS + 2, :]
         sc = jnp.where(row2 == C0 + j, 1.0 / uu, scale[...])
@@ -385,21 +422,6 @@
         coef[...] = jnp.where(
             row2 < K + STEPS, c * sc * inv_n, jnp.where(row2 == 30, inv_n, total)
         )
-
-        @pl.when(j < STEPS - 1)
-        def _():
-            wait_recv(cs)
-            slot = 2 + par
-            assemble(temp, wbuf[par, 0], mx.at[par], my.at[par], mc.at[par], 0, 0, 0)
-            fields[C0 + 1 + j, 0] = temp[...]
-            assemble_zones(slot)
-            fields[C0 + 1 + j, 1] = jnp.where(
-                lane3 == Z - 1, zext[0], jnp.where(lane3 == 0, zext[1], 0.0)
-            )
-
-        @pl.when(j == STEPS - 1)
-        def _():
-            fields[C0 + STEPS, 0, 1 : X + 1, 0:Y, :] = wbuf[par, 0]
 
         def update(p, carry):
             z, x = lax.div(p, X + 2), lax.rem(p, X + 2)
@@ -484,36 +506,39 @@
         K, X, Y, Z = recycled.shape
         NF = K + 2
         FR, ER, XR = round_up(NF * X, 8), round_up(NF, 8), round_up(X, 8)
-        groups = []
-        for g in GROUPS:
+        def count(group):
             n = 1
-            for a in g:
+            for a in group:
                 n *= mesh.shape[a]
-            groups.append(n)
-        biggest = max(groups)
+            return n
+
+        groups = ONE if count(AXES) <= 64 else TWO
+        n_two, n_step = [count(g) for g in TWO], [count(g) for g in groups]
+        biggest = max(n_two + n_step)
+        nc = (NF + CHUNK - 1) // CHUNK
         GR = round_up(K + 1, 8)
         V = lambda *s: pltpu.VMEM(s, jnp.float32)
         vm = pl.BlockSpec(memory_space=pltpu.VMEM)
         shape = jax.ShapeDtypeStruct((X, Y, Z), jnp.float32)
         return pl.pallas_call(
-            functools.partial(kernel, sizes),
+            functools.partial(kernel, sizes, groups),
             out_shape=(shape, shape, jax.ShapeDtypeStruct((STEPS + 1, STEPS), jnp.float32)),
             in_specs=[vm] * 4,
             out_specs=(vm, vm, vm),
             scratch_shapes=[
                 V(NF, X, Y, Z), V(NF, X, Y, Z),
                 V(2, 2, FR, Z), V(2, 2, 2, ER, Z),
-                V(2, 2, 1, X, Y, Z), V(2, 2, 2, XR, Z), V(2, 2, 2, 2, 8, Z),
+                V(2, 2, 1, X, Y, Z), V(2, 2, 2, XR, Z), V(2, 2, 2, 2, 1, Z),
                 V(2, 2, NF, Y, Z), V(2, 2, FR, Z), V(2, 2, 2, ER, Z),
-                V(4, 2, 1, X, Y, Z), V(4, 2, 2, 1, Y, Z), V(4, 2, 2, XR, Z), V(4, 2, 2, 2, 8, Z),
-                V(2, 2, 1, Y, Z), V(2, 2, XR, Z), V(2, 2, 2, 8, Z),
-                V(2, 1, X, Y, Z), V(2, 2, XR, Z), V(2, 2, 2, 8, Z),
+                V(4, 2, 1, X, Y, Z), V(4, 2, 2, 1, Y, Z), V(4, 2, 2, XR, Z), V(4, 2, 2, 2, 1, Z),
+                V(2, 2, 1, Y, Z), V(2, 2, XR, Z), V(2, 2, 2, 1, Z),
+                V(2, 1, X, Y, Z), V(2, 2, XR, Z), V(2, 2, 2, 1, Z),
                 V(K + STEPS + 1, 2, X + 2, Y + 8, Z), V(2, X + 2, Y + 8, Z), V(X, Y, Z),
                 V(X + 2, Y + 8, Z), V(2, X + 2, Y + 8, Z),
-                V(K + 1, GR, Z), V(groups[0], GR, Z), V(groups[1], GR, Z),
-                V(2, groups[0], 8, Z), V(2, groups[1], 8, Z),
+                V(K + 1, GR, Z), V(n_two[0], 8, Z), V(n_two[1], 8, Z),
+                V(2, n_step[0], 1, Z), V(2, n_step[-1], 1, Z),
                 V(32, Z), V(32, Z), V(32, Z), V(32, Z), V(K, Z),
-                pltpu.SemaphoreType.DMA((4, 26)), pltpu.SemaphoreType.DMA((4, 26)),
+                pltpu.SemaphoreType.DMA((2 * nc + 4, 26)), pltpu.SemaphoreType.DMA((2 * nc + 4, 26)),
                 pltpu.SemaphoreType.DMA((3, 2, biggest)), pltpu.SemaphoreType.DMA((3, 2, biggest)),
             ],
             compiler_params=pltpu.CompilerParams(collective_id=0, has_side_effects=True),

time: 104 us -> 86.2 us (0.83)
  Pallas kernels: 100 us -> 81.9 us
    pallas_call x1, Pallas kernels: 100 us -> 81.9 us  [body(): pl.pallas_call(functools.partial(kernel, sizes, groups), out_shape=(shape...]
where the time goes in v2:
time: 86.2 us; the launch traced here: 85.9 us
  Pallas kernels  81.9 us (95%)
  local copies, waits for them, and re-layouts  3.36 us (4%)
    pallas_call x1, Pallas kernels, body(): pl.pallas_call(functools.partial(kernel, sizes, groups), out_shape=(shape...  81.9 us
    unnamed x4, local copies, waits for them, and re-layouts  2 us

profile of v2, /device:TPU:0, one launch (start us, length us, event | category | flops | bytes accessed | tf_op | source)
XLA Modules:
  0.0 85.9 jit_solution(16429469153252476414)
XLA Ops:
  0.6 81.9 %shard_map.67 = (f32[4,16,128]{2,1,0:T(8,128)}, f32[4,16,128]{2,1,0:T(8,128)}, f32[9,8]{1,0:T(8,128)}) custom-call(f32[4,16,128]{2,1,0:T(8,128)} %rhs.1, f32[4,16,128]{2,1,0:T(8,128)} %guess.1, f32[4,16,128]{2,1,0:T(8,128)} %cond.1, f32[16,4,16,128]{3,2,1,0:T(8,128)} %rec.1), custom_call_target="tpu_custom_call" | custom-call | tf_op jit(solution)/shard_map/pallas_call | solution.py:523
  82.6 1.4 %copy.7 = f32[9,8]{0,1:T(8,128)} copy(f32[9,8]{1,0:T(8,128)} %get-tuple-element.5) | data formatting | bytes 576 | tf_op jit(solution)/shard_map/pallas_call | solution.py:523
  83.9 0.0 copy-start
  83.9 1.4 %copy.10 = f32[4,16,128]{2,1,0:T(8,128)} copy(f32[4,16,128]{2,1,0:T(8,128)} %get-tuple-element.9) | data formatting | bytes 65536
  85.3 0.0 copy-done
  85.3 0.6 copy.11
Async XLA Ops:
  83.9 1.4 %copy-start = (f32[4,16,128]{2,1,0:T(8,128)S(1)}, f32[4,16,128]{2,1,0:T(8,128)}, u32[]{:S(2)}) copy-start(f32[4,16,128]{2,1,0:T(8,128)} %get-tuple-element.10) | copy-start | bytes 98308

commit v3 on v2

--- a/solution.py
+++ b/solution.py
@@ -212,7 +212,7 @@
             buf = bufs[g]
             buf[rank] = total
             cs = []
-            for k in range(1, n):
+            for k in sorted(range(1, n), key=lambda k: -min(k, n - k)):
                 c = pltpu.make_async_remote_copy(
                     src_ref=buf.at[rank], dst_ref=buf.at[rank],
                     send_sem=rsend.at[slot, g, k], recv_sem=rrecv.at[slot, g, k],
@@ -228,9 +228,10 @@
                     send_sem=rsend.at[slot, g, k], recv_sem=rrecv.at[slot, g, k],
                     device_id=member(group, lax.rem(rank + k, n)), device_id_type=MESH,
                 ).wait_recv()
-            total = buf[0]
-            for r in range(1, n):
-                total = total + buf[r]
+            parts = [buf[r] for r in range(n)]
+            while len(parts) > 1:
+                parts = [sum(parts[r : r + 2][1:], parts[r]) for r in range(0, len(parts), 2)]
+            total = parts[0]
             for k, c in cs:
                 c.wait_send()
         return total
@@ -254,7 +255,7 @@
             pl.semaphore_signal(barrier, inc=1, device_id=target(d), device_id_type=MESH)
 
         count = count + ok.astype(jnp.int32)
-    for group in sorted(set(TWO + groups)):
+    for group in TWO:
         n, rank = group_info(group)
         for k in range(1, n):
             pl.semaphore_signal(
@@ -308,7 +309,7 @@
             img[K] = v
             pack_faces(v, bface.at[1], bedge.at[1], K * X, K)
         else:
-            lax.fori_loop(c * CHUNK, (c + 1) * CHUNK, image, 0)
+            lax.fori_loop(c * CHUNK, (c + 1) * CHUNK, image, 0, unroll=2)
         start_halo(second[c])
     pack_lanes(lambda f: img[f], K + 1, 1)
     start_halo(second[NC])
@@ -324,7 +325,7 @@
         gpart[a] = jnp.concatenate(rows, axis=0)
         return carry
 
-    lax.fori_loop(0, K + 1, gram_part, 0)
+    lax.fori_loop(0, K + 1, gram_part, 0, unroll=2)
     lane_g = lax.broadcasted_iota(jnp.int32, (GR, Z), 1)
     gram = jnp.zeros((GR, Z), f32)
     for a in range(K + 1):
@@ -339,7 +340,7 @@
             fields[f, 1] = zone_field(f)
             return carry
 
-        lax.fori_loop(0, K + 1, extend, 0)
+        lax.fori_loop(0, K + 1, extend, 0, unroll=4)
 
     part = gram[:8]
     for q in range(1, GR // 8):
@@ -433,7 +434,7 @@
             fields[C0 + 1 + j, z, x] = v + v2
             return carry
 
-        lax.fori_loop(0, 2 * (X + 2), update, 0)
+        lax.fori_loop(0, 2 * (X + 2), update, 0, unroll=4)
 
         @pl.when(j < STEPS - 1)
         def _():
@@ -495,6 +496,12 @@
     res_out[...] = res
 
 
+def deliver(sol, res, hes, sol_out, res_out, hes_out):
+    sol_out[...] = sol[...]
+    res_out[...] = res[...]
+    hes_out[...] = hes[...]
+
+
 def round_up(n, m):
     return (n + m - 1) // m * m
 
@@ -520,7 +527,7 @@
         V = lambda *s: pltpu.VMEM(s, jnp.float32)
         vm = pl.BlockSpec(memory_space=pltpu.VMEM)
         shape = jax.ShapeDtypeStruct((X, Y, Z), jnp.float32)
-        return pl.pallas_call(
+        sol, res, hes = pl.pallas_call(
             functools.partial(kernel, sizes, groups),
             out_shape=(shape, shape, jax.ShapeDtypeStruct((STEPS + 1, STEPS), jnp.float32)),
             in_specs=[vm] * 4,
@@ -543,6 +550,12 @@
             ],
             compiler_params=pltpu.CompilerParams(collective_id=0, has_side_effects=True),
         )(right_side, start_guess, conductivity, recycled)
+        return pl.pallas_call(
+            deliver,
+            out_shape=(shape, shape, jax.ShapeDtypeStruct(hes.shape, hes.dtype)),
+            in_specs=[vm] * 3,
+            out_specs=(vm,) * 3,
+        )(sol, res, hes)
 
     return jax.shard_map(
         body,

time: 86.2 us -> 84.8 us (0.984)
  local copies, waits for them, and re-layouts: 3.36 us -> 1.36 us
    unnamed x4 -> x0, local copies, waits for them, and re-layouts: 2 us -> none
    pallas_call x0 -> x1, Pallas kernels: none -> 1.41 us  [body(): pl.pallas_call(deliver, out_shape=(shape, shape, jax.ShapeDtypeStruct(hes...]
where the time goes in v3:
time: 84.8 us; the launch traced here: 84.5 us
  Pallas kernels  82.5 us (97%)
  local copies, waits for them, and re-layouts  1.36 us (2%)
    pallas_call x1, Pallas kernels, body(): pl.pallas_call(functools.partial(kernel, sizes, groups), out_shape=(shape...  81.1 us

profile of v3, /device:TPU:0, one launch (start us, length us, event | category | flops | bytes accessed | tf_op | source)
XLA Modules:
  0.0 84.5 jit_solution(14292586052206212876)
XLA Ops:
  0.6 81.1 %shard_map.67 = (f32[4,16,128]{2,1,0:T(8,128)}, f32[4,16,128]{2,1,0:T(8,128)}, f32[9,8]{1,0:T(8,128)}) custom-call(f32[4,16,128]{2,1,0:T(8,128)} %rhs.1, f32[4,16,128]{2,1,0:T(8,128)} %guess.1, f32[4,16,128]{2,1,0:T(8,128)} %cond.1, f32[16,4,16,128]{3,2,1,0:T(8,128)} %rec.1), custom_call_target="tpu_custom_call" | custom-call | tf_op jit(solution)/shard_map/pallas_call | solution.py:530
  81.8 1.4 %shard_map.68 = (f32[4,16,128]{2,1,0:T(8,128)}, f32[4,16,128]{2,1,0:T(8,128)}, f32[9,8]{1,0:T(8,128)}) custom-call(f32[4,16,128]{2,1,0:T(8,128)} %get-tuple-element.6.sol, f32[4,16,128]{2,1,0:T(8,128)} %get-tuple-element.7.res, f32[9,8]{1,0:T(8,128)} %get-tuple-element.8.hes), custom_call_target="tpu_custom_call" | custom-call | tf_op jit(solution)/shard_map/pallas_call | solution.py:553
  83.2 1.4 %copy.7 = f32[9,8]{0,1:T(8,128)} copy(f32[9,8]{1,0:T(8,128)} %get-tuple-element.11) | data formatting | bytes 576 | tf_op jit(solution)/shard_map/pallas_call | solution.py:553
